TPU v7x, 32 devices: a 4x4x1 block of a 4x4x8 slice. The times are simulated.
32 devices in a mesh: dp: 2 (over z, core), ep: 16 (over x, y).
Axes of the slice: x: 4, y: 4, z: 1, core: 2. Of those that a mesh axis runs over, the one named last changes fastest.
The devices are a block of a 4x4x8 slice.
Arguments:
- x: bfloat16 [2, 16, 256, 3072], P('dp', 'ep'), parts along dimension 0
- expert: int32 [2, 16, 256, 4], P('dp', 'ep'), parts along dimension 0
- slot: int32 [2, 16, 256, 4], P('dp', 'ep'), parts along dimension 0
- gate: float32 [2, 16, 256, 4], P('dp', 'ep'), parts along dimension 0
- w_gate: bfloat16 [16, 3072, 10752], P('ep')
- w_up: bfloat16 [16, 3072, 10752], P('ep')
- w_down: bfloat16 [16, 10752, 3072], P('ep')
Outputs:
- y: bfloat16 [2, 16, 256, 3072], P('dp', 'ep'), parts along dimension 0
There are 2 independent parts. A program takes and returns all parts, laid end to end along the dimension named above; an argument that names none is the same for every part.
All inputs are finite; a program needn't handle non-finite values.
Results may differ from a plain program's by a relative error of at most 0.009.
Values are sent between devices in bfloat16 or wider.
A program may use at most 768 MiB of HBM per device.

v0:
```python
import functools
import math

import jax
import jax.numpy as jnp
from jax import lax
from jax.experimental import pallas as pl
from jax.experimental.pallas import tpu as pltpu
from jax.sharding import PartitionSpec as P

MESH = pl.DeviceIdType.MESH
F32, BF16 = jnp.float32, jnp.bfloat16
COLS = 256
HELD = 6
OWN = 12
LAG = 2


def plan(side):
    far = lambda v: min(v, side - v)
    peers = sorted(((far(a) + far(b), a, b) for a in range(side) for b in range(side)))
    near = [(a, b) for n, a, b in peers if n <= 1]
    mid = [(a, b) for n, a, b in peers if n == 2]
    mid.sort(key=lambda o: (2 * o[0] == side, o[0], o[1] if o[0] == 1 else -o[1]))
    rest = [(a, b) for n, a, b in peers if n > 2]
    rest.sort(key=lambda o: (-far(o[0]) - far(o[1]), -far(o[0])))
    return near, mid, rest


def kernel(
    side, slots, x_ref, expert_ref, slot_ref, gate_ref, wg_ref, wu_ref, wd_ref, y_ref,
    z, h, back, kept, w, comb, x_sem, w_sem, y_sem, out_s, out_r, far_s, far_r, mid_s, mid_r, near_s, near_r,
):
    tokens, d = x_ref.shape
    ff = wd_ref.shape[0]
    near, mid, rest = plan(side)
    order = near + mid + rest
    where = {o: p for p, o in enumerate(order)}
    mirror = [where[(-a) % side, (-b) % side] for a, b in order]
    members = len(order)
    n_near, n_end = len(near), len(near) + len(mid)
    rows = lambda lo, hi: pl.ds(lo * slots, (hi - lo) * slots)
    me = lax.axis_index("ep")
    my_x, my_y = me // side, lax.rem(me, side)

    def device(p):
        a, b = order[p]
        return {"ep": lax.rem(my_x + a, side) * side + lax.rem(my_y + b, side)}

    x_at = h.at[pl.ds(n_near * slots, tokens), pl.ds(d, d)]
    x_copy = pltpu.make_async_copy(x_ref, x_at, x_sem)
    x_copy.start()

    barrier = pltpu.get_barrier_semaphore()
    for p in range(1, members):
        pl.semaphore_signal(barrier, inc=1, device_id=device(p), device_id_type=MESH)

    def hidden(lo, hi):
        down_by = n_end - n_near if lo >= n_end else 0
        return rows(lo - down_by, hi - down_by)

    def staged(p):
        if p < n_near:
            return h.at[rows(n_near + p - 1, n_near + p), pl.ds(2 * d, d)]
        if p < n_end:
            return kept.at[rows(p - n_near, p - n_near + 1)]
        return h.at[hidden(p, p + 1), pl.ds(0, d)]

    n_up, n_down = ff // COLS, d // COLS

    def start(place, q):
        gap = 4 * ff - 2 * HELD * d
        upper = (gap if place >= HELD // 2 else 0) if isinstance(place, int) else jnp.where(place >= HELD // 2, gap, 0)
        return pl.multiple_of((2 * place + q) * d + upper, COLS)

    def fetch_up(tile, place):
        at = pl.ds(pl.multiple_of(tile * COLS, COLS), COLS)
        for q, ref in enumerate((wg_ref, wu_ref)):
            pltpu.make_async_copy(ref.at[:, at], w.at[pl.ds(start(place, q), d)], w_sem.at[place]).start()

    def fetch_down(pair, place):
        for q in range(2):
            at = pl.ds(pl.multiple_of((2 * pair + q) * COLS, COLS), COLS)
            pltpu.make_async_copy(wd_ref.at[:, at], w.at[down_rows(place, q)], w_sem.at[HELD + place]).start()

    def down_rows(place, q):
        return pl.ds(pl.multiple_of((2 * place + q) * ff, COLS), ff)

    def wait_for(got, sem):
        with jax.named_scope("weights"):
            pltpu.make_async_copy(got, got, sem).wait()

    def fetched(place):
        wait_for(w.at[pl.ds(start(place, 0), 2 * d)], w_sem.at[place])

    def loop(lo, hi, body):
        def step(i, carry):
            body(i)
            return carry

        lax.fori_loop(lo, hi, step, 0)

    expert, slot = expert_ref[...], slot_ref[...]
    off = lax.rem(expert // side - my_x + side, side) * side + lax.rem(lax.rem(expert, side) - my_y + side, side)
    place = jnp.zeros_like(off)
    for p, (a, b) in enumerate(order):
        place = jnp.where(off == a * side + b, p, place)
    code = jnp.where(slot < slots, place * slots + slot, -1)
    gate = gate_ref[...].astype(BF16).astype(F32)

    def chosen(lo, n, value):
        row = lax.broadcasted_iota(jnp.int32, (n, tokens), 0) + lo
        out = jnp.zeros((n, tokens), F32)
        for j in range(code.shape[0]):
            out = jnp.where(row == code[j : j + 1, :], value(j), out)
        return out

    def picked(lo, hi):
        return chosen(lo * slots, (hi - lo) * slots, lambda j: 1.0).astype(BF16)

    def block_rows(lo, hi, pick, at, half=None):
        first, end = (0, d) if half is None else (half * d // 2, (half + 1) * d // 2)
        for c in range(first, end, 2 * COLS):
            cols = pl.ds(c, min(2 * COLS, end - c))
            got = jnp.dot(pick, x_at[:, cols], preferred_element_type=F32).astype(BF16)
            for p in range(lo, hi):
                at(p)[:, cols] = got[(p - lo) * slots : (p - lo + 1) * slots]

    def send(p, half=None):
        cols = pl.ds(0, d) if half is None else pl.ds(half * d // 2, d // 2)
        return pltpu.make_async_remote_copy(
            src_ref=staged(p).at[:, cols],
            dst_ref=z.at[rows(mirror[p], mirror[p] + 1), cols],
            send_sem=out_s.at[p],
            recv_sem=out_r.at[mirror[p]],
            device_id=device(p),
            device_id_type=MESH,
        )

    def arrived(lo, hi):
        for p in range(lo, hi):
            got = z.at[rows(p, p + 1)]
            with jax.named_scope(f"arrive{p}"):
                pltpu.make_async_copy(got, got, out_r.at[p]).wait()

    with jax.named_scope("x"):
        x_copy.wait()
    for i in range(HELD - 1):
        fetch_up(i, i)
    pick = picked(1, n_near)
    block_rows(1, n_near, pick, staged, 0)
    with jax.named_scope("barrier"):
        pl.semaphore_wait(barrier, members - 1)
    for p in range(1, n_near):
        send(p, 0).start()
    block_rows(1, n_near, pick, staged, 1)
    for p in range(1, n_near):
        send(p, 1).start()
    with jax.named_scope("rows"):
        block_rows(n_end, members, picked(n_end, members), staged)
        block_rows(n_near, n_end, picked(n_near, n_end), staged)
        block_rows(0, 1, picked(0, 1), lambda p: z.at[rows(0, 1)])
    for c in range(0, members * slots, 128):
        part = chosen(c, 128, lambda j: gate[j : j + 1, :])
        comb[:, pl.ds(c, 128)] = part.T.astype(BF16)

    def up(lo, hi, tile, place, n):
        for k in range(n):
            g, u = (
                jnp.dot(z[rows(lo, hi), :], w[pl.ds(start(place + k, q), d), :], preferred_element_type=F32)
                for q in range(2)
            )
            cols = pl.ds(pl.multiple_of((tile + k) * COLS, COLS), COLS)
            h[hidden(lo, hi), cols] = (jax.nn.silu(g) * u).astype(BF16)

    def own_step(j):
        place = j - jnp.where(j >= HELD, HELD, 0)
        fetched(place)
        later = j + HELD - 1

        @pl.when(later < OWN)
        def _():
            fetch_up(later, later - jnp.where(later >= HELD, HELD, 0))

        with jax.named_scope("own"):
            up(0, 1, j, place, 1)

    def thirds(lo, hi, body):
        def outer(o, carry):
            loop(0, 3, lambda r: body(3 * o + r, r, jnp.where(r == 0, 2, r - 1)))
            return carry

        lax.fori_loop(lo // 3, hi // 3, outer, 0)

    turn = OWN - HELD
    wrap = n_up - turn

    def near_steps(lo, hi, first, back_by):
        def body(i, r, r_ahead):
            if lo:
                for k in range(2):
                    fetched(2 * r + k)
            later = 2 * i + 4
            tile = later + turn - jnp.where(later >= n_up, n_up + turn, jnp.where(later >= wrap, n_up, 0))
            for k in range(2):

                @pl.when((i >= 1) & (later + k <= n_up + 2))
                def _():
                    fetch_up(tile + k, 2 * r_ahead + k)

            with jax.named_scope("near_up"):
                up(first, n_near, 2 * i + turn - back_by, 2 * r, 2)

        thirds(lo, hi, body)

    def later_steps(lo, hi):
        def body(i):
            half = lax.rem(i, 2)
            for k in range(3):
                fetched(3 * half + k)

            @pl.when(3 * i + 3 < n_up)
            def _():
                for k in range(3):
                    fetch_up(3 * i + 3 + k, 3 - 3 * half + k)

            @pl.when(3 * i + 3 >= n_up)
            def _():
                fetch_down(0, 0)

            with jax.named_scope("up"):
                up(lo, hi, 3 * i, 3 * half, 3)

        loop(0, n_up // 3, body)

    def fetch_three_up():
        for k in range(HELD // 2):
            fetch_up(k, k)

    n_pairs = n_down // 2

    def down_steps(lo, hi, body, after=None):
        def step(i):
            place = lax.rem(i, 2)
            wait_for(w.at[pl.ds(pl.multiple_of(2 * place * ff, COLS), 2 * ff)], w_sem.at[HELD + place])

            @pl.when(i + 1 < n_pairs)
            def _():
                fetch_down(i + 1, 1 - place)

            if after:
                pl.when(i + 1 == n_pairs)(after)
            with jax.named_scope("down"):
                body(i, place)

        loop(lo, hi, step)

    def result(p, c, n, send_sem, recv_sem):
        cols = pl.ds(pl.multiple_of(c * COLS, COLS), n * COLS)
        return pltpu.make_async_remote_copy(
            src_ref=z.at[rows(p, p + 1), cols],
            dst_ref=back.at[rows(mirror[p], mirror[p] + 1), cols],
            send_sem=send_sem,
            recv_sem=recv_sem,
            device_id=device(p),
            device_id_type=MESH,
        )

    def send_results(lo, hi, c, n, piece, send_sem, recv_sem):
        for p in range(lo, hi):
            result(p, c, n, send_sem, recv_sem.at[piece]).start()

    def results_arrived(lo, hi, c, n, piece, recv_sem, name):
        got = back.at[rows(lo, hi), pl.ds(pl.multiple_of(c * COLS, COLS), n * COLS)]
        with jax.named_scope(name):
            pltpu.make_async_copy(got, got, recv_sem.at[piece]).wait()

    def chunk(c):
        return pl.ds(pl.multiple_of(c * COLS, COLS), COLS)

    def product(lo, hi, place, q):
        lhs = h[hidden(lo, hi), :]
        return jnp.dot(lhs, w[down_rows(place, q), :], preferred_element_type=F32).astype(BF16)

    def down(lo, hi):
        def body(i, place):
            for q in range(2):
                z[rows(lo, hi), chunk(2 * i + q)] = product(lo, hi, place, q)

        return body

    def down_near(i, place):
        for q in range(2):
            out = product(0, n_near, place, q)
            back[rows(0, 1), chunk(2 * i + q)] = out[:slots]
            z[rows(1, n_near), chunk(2 * i + q)] = out[slots:]

    def write(c, n):
        cols = pl.ds(pl.multiple_of(c * COLS, COLS), n * COLS)
        return pltpu.make_async_copy(back.at[pl.ds(0, tokens), cols], y_ref.at[:, cols], y_sem)

    def add_up(c, n):
        cols = pl.ds(pl.multiple_of(c * COLS, COLS), n * COLS)
        total = jnp.dot(comb[...], back[:, cols], preferred_element_type=F32)
        back[pl.ds(0, tokens), cols] = total.astype(BF16)

    def near_and_add(i, place):
        add_up(2 * (i - LAG), 2)
        down_near(i, place)
        write(2 * (i - LAG), 2).start()

    loop(0, OWN, own_step)
    arrived(1, n_near)
    for p in range(n_end, members):
        send(p).start()
    near_steps(0, HELD // 2, 1, 0)
    near_steps(HELD // 2, wrap // 2, 0, 0)
    near_steps(wrap // 2, n_up // 2, 1, n_up)
    arrived(n_end, members)
    for p in range(n_near, n_end):
        send(p).start()
    with jax.named_scope("sent_near_rest"):
        for p in [*range(1, n_near), *range(n_end, members)]:
            send(p).wait_send()
    later_steps(n_end, members)
    down_steps(0, n_pairs, down(n_end, members), fetch_three_up)
    for p in range(n_end, members):
        result(p, 0, n_down, far_s, far_r).start()
    arrived(n_near, n_end)
    with jax.named_scope("sent_mid"):
        for p in range(n_near, n_end):
            send(p).wait_send()
    later_steps(n_near, n_end)

    def mid_step(i, place):
        down(n_near, n_end)(i, place)
        send_results(n_near, n_end, 2 * i, 2, i, mid_s, mid_r)

    down_steps(0, n_pairs, mid_step, lambda: fetch_down(0, 0))

    def send_near(i):
        send_results(1, n_near, 2 * i, 2, i, near_s, near_r)

    def near_step(i, place):
        down_near(i, place)
        send_near(i)

    def arrived_back(i):
        results_arrived(n_near, n_end, 2 * i, 2, i, mid_r, "mid")
        results_arrived(1, n_near, 2 * i, 2, i, near_r, "near")

    def near_step_and_add(i, place):
        arrived_back(i - LAG)
        near_and_add(i, place)
        send_near(i)

    def last_step(i, place):
        def one(q):
            z[rows(1, n_near), chunk(2 * i + q)] = product(1, n_near, place, q)
            send_results(1, n_near, 2 * i + q, 1, n_pairs - 1 + q, near_s, near_r)

        loop(0, 2, one)
        for q in range(2):
            back[rows(0, 1), chunk(2 * i + q)] = product(0, 1, place, q)

    down_steps(0, LAG, near_step)
    got = back.at[rows(n_end, members)]
    with jax.named_scope("far"):
        pltpu.make_async_copy(got, got, far_r).wait()
    down_steps(LAG, n_pairs - 1, near_step_and_add)
    down_steps(n_pairs - 1, n_pairs, last_step)
    for i in range(n_pairs - 1 - LAG, n_pairs - 1):
        arrived_back(i)
        add_up(2 * i, 2)
        write(2 * i, 2).start()
    results_arrived(n_near, n_end, n_down - 2, 2, n_pairs - 1, mid_r, "mid")
    for q in range(2):
        results_arrived(1, n_near, n_down - 2 + q, 1, n_pairs - 1 + q, near_r, "near")
        add_up(n_down - 2 + q, 1)
        write(n_down - 2 + q, 1).start()
    with jax.named_scope("written"):
        for i in range(n_pairs - 1):
            write(2 * i, 2).wait()
        for q in range(2):
            write(n_down - 2 + q, 1).wait()
    gone = z.at[rows(n_end, members)]
    pltpu.make_async_copy(gone, gone, far_s).wait()
    gone = z.at[rows(n_near, n_end)]
    pltpu.make_async_copy(gone, gone, mid_s).wait()
    gone = z.at[rows(1, n_near)]
    pltpu.make_async_copy(gone, gone, near_s).wait()


def solution(mesh):
    members = mesh.shape["ep"]
    side = math.isqrt(members)

    def layer(x, expert, slot, gate, w_gate, w_up, w_down):
        tokens, d = x.shape[2:]
        ff, top = w_gate.shape[2], expert.shape[3]
        slots = 5 * tokens * top // (4 * members)
        total = members * slots
        n_near, n_mid, n_rest = map(len, plan(side))
        any_ = pl.BlockSpec(memory_space=pl.ANY)
        vmem = pl.BlockSpec(memory_space=pltpu.VMEM)
        turned = lambda v: v.reshape(tokens, top).T
        y = pl.pallas_call(
            functools.partial(kernel, side, slots),
            out_shape=jax.ShapeDtypeStruct((tokens, d), BF16),
            in_specs=[any_, vmem, vmem, vmem, any_, any_, any_],
            out_specs=any_,
            scratch_shapes=[
                pltpu.VMEM((total, d), BF16),
                pltpu.VMEM(((n_near + max(n_mid, n_rest)) * slots, ff), BF16),
                pltpu.VMEM((total, d), BF16),
                pltpu.VMEM((n_mid * slots, d), BF16),
                pltpu.VMEM((4 * ff, COLS), BF16),
                pltpu.VMEM((tokens, total), BF16),
                pltpu.SemaphoreType.DMA,
                pltpu.SemaphoreType.DMA((HELD + 2,)),
                pltpu.SemaphoreType.DMA,
                pltpu.SemaphoreType.DMA((members,)),
                pltpu.SemaphoreType.DMA((members,)),
                pltpu.SemaphoreType.DMA,
                pltpu.SemaphoreType.DMA,
                pltpu.SemaphoreType.DMA,
                pltpu.SemaphoreType.DMA((d // COLS,)),
                pltpu.SemaphoreType.DMA,
                pltpu.SemaphoreType.DMA((d // COLS,)),
            ],
            compiler_params=pltpu.CompilerParams(
                collective_id=0, has_side_effects=True, vmem_limit_bytes=67_043_328
            ),
            name="moe",
        )(
            x.reshape(tokens, d), turned(expert), turned(slot), turned(gate),
            w_gate.reshape(d, ff), w_up.reshape(d, ff), w_down.reshape(ff, d),
        )
        return y.reshape(1, 1, tokens, d)

    per_device, per_expert = P("dp", "ep", None, None), P("ep", None, None)
    return jax.shard_map(
        layer,
        mesh=mesh,
        in_specs=(per_device,) * 4 + (per_expert,) * 3,
        out_specs=per_device,
        check_vma=False,
    )
```

profile of v0, /device:TPU:97, one launch (start us, length us, event | category | flops | bytes accessed | tf_op | source)
XLA Modules:
  0.0 298.4 jit_solution(16027482474908202405)
XLA Ops:
  0.0 295.8 %moe.1 = bf16[256,3072]{1,0:T(8,128)(2,1)} custom-call(bf16[256,3072]{1,0:T(8,128)(2,1)} %bitcast.18, s32[4,256]{1,0:T(4,128)} %bitcast.19, s32[4,256]{1,0:T(4,128)} %bitcast.20, f32[4,256]{1,0:T(4,128)} %bitcast.21, bf16[3072,10752]{1,0:T(8,128)(2,1)} %bitcast.14, bf16[3072,10752]{1,0:T(8,128)(2,1)} %bitcast.15, bf16[10752,3072]{1,0:T(8,128)(2,1)} %bitcast.16), custom_call_target="tpu_custom_call" | custom-call | tf_op jit(solution)/shard_map/moe/pallas_call | solution.py:407
  295.8 2.7 copy.9
where the time goes:
time: 299 us; the launch traced here: 298 us
  Pallas kernels  296 us (99%)
    pallas_call x1, Pallas kernels, layer(): pl.pallas_call(functools.partial(kernel, side, slots), out_shape=jax.Shap...  296 us

commit v1 on v0

--- a/solution.py
+++ b/solution.py
@@ -13,7 +13,7 @@
 COLS = 256
 HELD = 6
 OWN = 12
-LAG = 2
+LAG = 3
 
 
 def plan(side):

time: 299 us -> 297 us (level)
  no operation moved by 1% of the time
where the time goes in v1:
time: 297 us
  Pallas kernels  294 us (99%)
    pallas_call x1, Pallas kernels, layer(): pl.pallas_call(functools.partial(kernel, side, slots), out_shape=jax.Shap...  294 us

profile of v1, /device:TPU:97, one launch (start us, length us, event | category | flops | bytes accessed | tf_op | source)
XLA Modules:
  0.0 296.7 jit_solution(5696886534656005468)
XLA Ops:
  0.0 294.0 %moe.1 = bf16[256,3072]{1,0:T(8,128)(2,1)} custom-call(bf16[256,3072]{1,0:T(8,128)(2,1)} %bitcast.18, s32[4,256]{1,0:T(4,128)} %bitcast.19, s32[4,256]{1,0:T(4,128)} %bitcast.20, f32[4,256]{1,0:T(4,128)} %bitcast.21, bf16[3072,10752]{1,0:T(8,128)(2,1)} %bitcast.14, bf16[3072,10752]{1,0:T(8,128)(2,1)} %bitcast.15, bf16[10752,3072]{1,0:T(8,128)(2,1)} %bitcast.16), custom_call_target="tpu_custom_call" | custom-call | tf_op jit(solution)/shard_map/moe/pallas_call | solution.py:407
  294.0 2.7 copy.9

commit v2 on v1

--- a/solution.py
+++ b/solution.py
@@ -13,7 +13,7 @@
 COLS = 256
 HELD = 6
 OWN = 12
-LAG = 3
+LAG = 4
 
 
 def plan(side):

time: 297 us -> 297 us (level)
  no operation moved by 1% of the time
where the time goes in v2:
time: 297 us
  Pallas kernels  294 us (99%)
    pallas_call x1, Pallas kernels, layer(): pl.pallas_call(functools.partial(kernel, side, slots), out_shape=jax.Shap...  294 us

profile of v2, /device:TPU:97, one launch (start us, length us, event | category | flops | bytes accessed | tf_op | source)
XLA Modules:
  0.0 296.8 jit_solution(13031459710806345873)
XLA Ops:
  0.0 294.1 %moe.1 = bf16[256,3072]{1,0:T(8,128)(2,1)} custom-call(bf16[256,3072]{1,0:T(8,128)(2,1)} %bitcast.18, s32[4,256]{1,0:T(4,128)} %bitcast.19, s32[4,256]{1,0:T(4,128)} %bitcast.20, f32[4,256]{1,0:T(4,128)} %bitcast.21, bf16[3072,10752]{1,0:T(8,128)(2,1)} %bitcast.14, bf16[3072,10752]{1,0:T(8,128)(2,1)} %bitcast.15, bf16[10752,3072]{1,0:T(8,128)(2,1)} %bitcast.16), custom_call_target="tpu_custom_call" | custom-call | tf_op jit(solution)/shard_map/moe/pallas_call | solution.py:407
  294.2 2.7 copy.9
